TPU v7x, 32 devices: a whole 2x2x4 slice. The times are simulated.
32 devices in a mesh: gx: 4 (over y, core), gy: 8 (over z, x).
Axes of the slice: x: 2, y: 2, z: 4, core: 2. Of those that a mesh axis runs over, the one named last changes fastest.
Arguments:
- hidden_states: bfloat16 [1024, 128], replicated, may hold values from -60 to 60
- item_table: bfloat16 [262144, 128], P(('gx', 'gy')), may hold values from -1.796875 to 1.796875
- targets: int32 [1024], replicated, may hold values from 0 to 262143
Outputs:
- expected: float32 [1024, 128], P(('gx', 'gy'))
- nll: float32 [1024], P(('gx', 'gy'))
All inputs are finite; a program needn't handle non-finite values.
Results may differ from a plain program's by a relative error of at most 0.0023.
Values sent between devices are 32-bit elements; how exact they have to be, the bound alone decides.
A program may use at most 64 MiB of HBM per device.

v0:
```python
import jax
import jax.numpy as jnp
from jax import lax
from jax.sharding import PartitionSpec as P

BLK = 512


def local(hidden_states, item_table, targets):
    positions = hidden_states.shape[0]
    shard_items = item_table.shape[0]
    nblocks = shard_items // BLK

    def visit_block(block_index, carry):
        highest, totals, weighted = carry
        block = lax.dynamic_slice_in_dim(item_table, block_index * BLK, BLK, 0)
        scores = lax.dot_general(
            hidden_states, block, (((1,), (1,)), ((), ())), preferred_element_type=jnp.float32
        )
        block_max = jnp.max(scores, axis=1)
        exponent = jnp.exp(scores - block_max[:, None])
        block_sum = jnp.sum(exponent, axis=1)
        probs_low = exponent.astype(jnp.bfloat16)
        block_acc = jnp.dot(probs_low, block, preferred_element_type=jnp.float32)
        new_max = jnp.maximum(highest, block_max)
        retain = jnp.exp(highest - new_max)
        rescale = jnp.exp(block_max - new_max)
        totals = totals * retain + block_sum * rescale
        weighted = weighted * retain[:, None] + block_acc * rescale[:, None]
        return (new_max, totals, weighted)

    start_state = (
        jnp.full((positions,), -1e30, jnp.float32),
        jnp.zeros((positions,), jnp.float32),
        jnp.zeros((positions, item_table.shape[1]), jnp.float32),
    )
    highest, totals, weighted = lax.fori_loop(0, nblocks, visit_block, start_state)
    device_index = lax.axis_index(("gx", "gy"))
    local_index = targets - device_index * shard_items
    owner_mask = (local_index >= 0) & (local_index < shard_items)
    target_rows = item_table[jnp.clip(local_index, 0, shard_items - 1)]
    own_logit = jnp.sum(hidden_states.astype(jnp.float32) * target_rows.astype(jnp.float32), axis=1)
    own_logit = jnp.where(owner_mask, own_logit, 0.0)
    row_count = positions // lax.axis_size(("gx", "gy"))
    first_row = device_index * row_count
    global_max = lax.pmax(highest, ("gx", "gy"))
    factor = jnp.exp(highest - global_max)
    weighted_rows, total_rows, target_part = (
        lax.psum_scatter(weighted * factor[:, None], ("gx", "gy"), scatter_dimension=0, tiled=True),
        lax.psum_scatter(totals * factor, ("gx", "gy"), scatter_dimension=0, tiled=True),
        lax.psum_scatter(own_logit, ("gx", "gy"), scatter_dimension=0, tiled=True),
    )
    max_rows = lax.dynamic_slice_in_dim(global_max, first_row, row_count, 0)
    expected = weighted_rows / total_rows[:, None]
    nll = max_rows + jnp.log(total_rows) - target_part
    return (expected, nll)


def solution(mesh):
    return jax.shard_map(
        local,
        mesh=mesh,
        in_specs=(P(), P(("gx", "gy"), None), P()),
        out_specs=(P(("gx", "gy"), None), P(("gx", "gy"))),
        check_vma=False,
    )
```

profile of v0, /device:TPU:0, one launch (start us, length us, event | category | flops | bytes accessed | tf_op | source)
XLA Modules:
  0.0 252.0 jit_solution(11066201469598881349)
XLA Ops:
  7.2 57.6 %while.18 = (s32[]{:T(128)}, f32[1024]{0:T(1024)S(1)}, f32[1024]{0:T(1024)S(1)}, f32[1024,128]{1,0:T(8,128)S(1)}, bf16[8192,128]{1,0:T(8,128)(2,1)}, /*index=5*/...) while((s32[]{:T(128)}, f32[1024]{0:T(1024)S(1)}, f32[1024]{0:T(1024)S(1)}, ...), condition=%wide.region_3.0_spmd.clone, body=%wide.region_0.0_spmd.clone.sunk | while | flops 271587328 | bytes 7921838 | solution.py:37
  7.3 1.5 fusion.25
  8.7 0.3 fusion.26
  9.1 1.8 fusion.28
  10.9 1.5 fusion.25
  12.3 0.3 fusion.26
  12.7 1.8 fusion.28
  14.5 1.5 fusion.25
  16.3 1.8 fusion.28
  18.1 1.5 fusion.25
  19.5 0.3 fusion.26
  19.9 1.8 fusion.28
  21.7 1.5 fusion.25
  23.1 0.3 fusion.26
  23.5 1.8 fusion.28
  25.3 1.5 fusion.25
  26.7 0.3 fusion.26
  27.1 1.8 fusion.28
  28.9 1.5 fusion.25
  30.7 1.8 fusion.28
  32.5 1.5 fusion.25
  34.3 1.8 fusion.28
  36.1 1.5 fusion.25
  37.9 1.8 fusion.28
  39.7 1.5 fusion.25
  41.1 0.3 fusion.26
  41.5 1.8 fusion.28
  43.3 1.5 fusion.25
  45.1 1.8 fusion.28
  46.9 1.5 fusion.25
  48.3 0.3 fusion.26
  48.7 1.8 fusion.28
  50.5 1.5 fusion.25
  52.3 1.8 fusion.28
  54.0 1.5 fusion.25
  55.9 1.8 fusion.28
  57.6 1.5 fusion.25
  59.5 1.8 fusion.28
  61.2 1.5 fusion.25
  62.7 0.3 fusion.26
  63.1 1.8 fusion.28
  64.8 42.0 %pmax.7 = f32[1024]{0:T(1024)S(1)} all-reduce(f32[1024]{0:T(1024)S(1)} %get-tuple-element.114), channel_id=1, replica_groups=mesh['gx'=4,'gy'=8] {'gx','gy'}, use_global_device_ids=true, to_apply=%region_4.5 | all-reduce | flops 1024 | bytes 8192 | tf_op jit(solution)/shard_map/pmax | solution.py:46
  106.9 1.0 broadcast_multiply_fusion
  107.9 4.7 %gather_fusion = bf16[1024,128]{1,0:T(8,128)(2,1)S(1)} fusion(bf16[8192,128]{1,0:T(8,128)(2,1)} %get-tuple-element.242, s32[1024]{0:T(1024)S(1)} %fusion.11), kind=kCustom, calls=%fused_computation | custom fusion | bytes 528384 | tf_op jit(solution)/shard_map/gather | solution.py:41
  112.9 40.2 %all-reduce.2 = (f32[1024]{0:T(1024)S(1)}, f32[1024]{0:T(1024)S(1)}) all-reduce(f32[1024]{0:T(1024)S(1)} %get-tuple-element.157, f32[1024]{0:T(1024)S(1)} %and_select_fusion), channel_id=3, replica_groups=mesh['gx'=4,'gy'=8] {'gx','gy'}, use_global_device_ids=true, to_apply=%region_6.7.clone | all-reduce | flops 2048 | bytes 16384
  153.1 0.6 dynamic-slice_subtract_fusion
  153.7 90.1 %reduce-scatter.2.cloned.1.call-done = f32[32,128]{1,0:T(8,128)} async-done(((f32[1024,128]{1,0:T(8,128)}), f32[32,128]{1,0:T(8,128)}) %reduce-scatter.2.cloned.1.call-update) | async-done | bytes 16400 | tf_op jit(solution)/shard_map/reduce_scatter | solution.py:49
  243.8 1.4 broadcast_divide_fusion
  (37 shorter events, 3.1 us)
Async XLA Ops:
  7.2 236.6 %reduce-scatter.2.cloned.1.call-start = ((), (), s32[]{:S(2)}) async-start(), calls=%async_computation.1 | async-start | bytes 540672 | tf_op jit(solution)/shard_map/reduce_scatter | solution.py:49
  7.2 100.7 %copy-start.1 = (s32[1024]{0:T(1024)S(1)}, s32[1024]{0:T(1024)}, u32[]{:S(2)}) copy-start(s32[1024]{0:T(1024)} %param.7) | copy-start | bytes 12292
  64.8 47.8 %copy-start = (bf16[1024,128]{1,0:T(8,128)(2,1)S(1)}, bf16[1024,128]{1,0:T(8,128)(2,1)}, u32[]{:S(2)}) copy-start(bf16[1024,128]{1,0:T(8,128)(2,1)} %get-tuple-element.241) | copy-start | bytes 786436
Sparse Core Ops, SparseCore 0:
  108.0 135.7 reduce-scatter.1
where the time goes:
time: 253 us; the launch traced here: 252 us
  waiting for transfers between devices  90.1 us (36%)
  blocking collectives  82.2 us (32%)
  matrix products  51.5 us (20%)
  between operations  14.1 us (6%)
  other arithmetic  8.69 us (3%)
  local copies, waits for them, and re-layouts  4.75 us (2%)
    reduce_scatter x1, waiting for transfers between devices, local(): lax.psum_scatter(weighted * factor[:, None], ('gx', 'gy'), scatter_dimens...  90.1 us
    pmax x1, blocking collectives, local(): global_max = lax.pmax(highest, ('gx', 'gy'))  42 us
    unnamed x1, blocking collectives  40.2 us
    dot_general x16, matrix products, visit_block(): block_acc = jnp.dot(probs_low, block, preferred_element_type=jnp.float32)  28 us
    dot_general x16, matrix products, visit_block(): lax.dot_general(hidden_states, block, (((1,), (1,)), ((), ())), preferred...  23.4 us
    reduce_sum x16, other arithmetic, visit_block(): block_sum = jnp.sum(exponent, axis=1)  5.24 us
  transfers between devices with their start and end apart: 1, of which 1 were waited for; matrix products, arithmetic and copies ran while one was open for 2% of the time, Pallas kernels for 0%

commit v1 on v0

v1 whole, which is shorter than its diff:
```python
import functools

import jax
import jax.numpy as jnp
from jax import lax
from jax.experimental import pallas as pl
from jax.experimental.pallas import tpu as pltpu
from jax.sharding import PartitionSpec as P

AXES = ("gx", "gy")
CHUNK = 256
BLOCK = 1024
SUB = 256
MESH = pl.DeviceIdType.MESH
NT = (((1,), (1,)), ((), ()))


def kernel(n, ngy, rows, hid, tab, tgt, exp_out, nll_out,
           tabt, s_even, s_odd, acc, send, recv, send_sem, recv_sem):
    positions, width = hid.shape
    items = tab.shape[0]
    nchunk = positions // CHUNK
    nblock = items // BLOCK
    per_chunk = CHUNK // rows
    stat_row = send.shape[1] - 8
    gx = lax.axis_index("gx")
    gy = lax.axis_index("gy")
    me = gx * ngy + gy

    barrier = pltpu.get_barrier_semaphore()

    def greet(k, c):
        other = lax.rem(me + k, n)
        pl.semaphore_signal(barrier, inc=1, device_id=(other // ngy, lax.rem(other, ngy)), device_id_type=MESH)
        return c

    lax.fori_loop(1, n, greet, 0)

    eye = (lax.broadcasted_iota(jnp.int32, (width, width), 0)
           == lax.broadcasted_iota(jnp.int32, (width, width), 1)).astype(jnp.float32).astype(jnp.bfloat16)

    def turn(i, c):
        at = pl.ds(pl.multiple_of(i * SUB, SUB), SUB)
        tabt[0:width, at] = lax.dot_general(eye, tab[at, :], NT, preferred_element_type=jnp.float32).astype(jnp.bfloat16)
        return c

    lax.fori_loop(0, items // SUB, turn, 0, unroll=4)
    tabt[width:, :] = jnp.ones((tabt.shape[0] - width, items), jnp.bfloat16)

    first = me // per_chunk + 1
    sub_iota = lax.broadcasted_iota(jnp.int32, (8, CHUNK), 0)

    def chunk_of(k):
        return lax.rem(first + k, nchunk)

    def score(chunk, block, s_ref):
        at = pl.multiple_of(chunk * CHUNK, CHUNK)
        states = hid[pl.ds(at, CHUNK), :]
        top = jnp.full((8, CHUNK), -jnp.inf, jnp.float32)
        for sub in range(BLOCK // SUB):
            base = pl.multiple_of(block * BLOCK + sub * SUB, SUB)
            s = lax.dot_general(tab[pl.ds(base, SUB), :], states, NT, preferred_element_type=jnp.float32)
            s_ref[sub * SUB:(sub + 1) * SUB, :] = s
            for g in range(SUB // 8):
                top = jnp.maximum(top, s[8 * g:8 * g + 8])
        return jnp.max(top, axis=0, keepdims=True)

    def soft(block, s_ref, top, highest, place, hit):
        new = jnp.maximum(highest, top)
        retain = jnp.exp(highest - new)
        here = place - block * BLOCK
        parts = []
        for g in range(BLOCK // 8):
            s = s_ref[8 * g:8 * g + 8, :]
            hit = jnp.where(here == 8 * g, s, hit)
        p = jnp.exp(s_ref[...] - new).astype(jnp.bfloat16)
        base = pl.multiple_of(block * BLOCK, BLOCK)
        acc[...] = acc[...] * retain + jnp.dot(tabt[:, pl.ds(base, BLOCK)], p, preferred_element_type=jnp.float32)
        return new, hit

    def pair(k, place, j, carry):
        top_even, highest, hit = carry
        chunk = chunk_of(k)
        top_odd = score(chunk, 2 * j + 1, s_odd)
        highest, hit = soft(2 * j, s_even, top_even, highest, place, hit)
        later = k * nblock + 2 * j + 2
        top_even = score(chunk_of(later // nblock), lax.rem(later, nblock), s_even)
        highest, hit = soft(2 * j + 1, s_odd, top_odd, highest, place, hit)
        return top_even, highest, hit

    def one_chunk(k, top_even):
        chunk = chunk_of(k)
        at = pl.multiple_of(chunk * CHUNK, CHUNK)
        place = tgt[0:1, pl.ds(at, CHUNK)] - me * items - sub_iota
        acc[...] = jnp.zeros_like(acc)
        top_even, highest, hit = lax.fori_loop(
            0, nblock // 2, functools.partial(pair, k, place),
            (top_even, jnp.full((1, CHUNK), -1e30, jnp.float32), jnp.zeros((8, CHUNK), jnp.float32)))
        weighted = acc[0:width, :].T
        stats = jnp.concatenate(
            [highest, acc[width:width + 1, :], jnp.sum(hit, axis=0, keepdims=True), jnp.zeros((5, CHUNK), jnp.float32)], axis=0)
        for o in range(per_chunk):
            owner = chunk * per_chunk + o
            send[owner, 0:rows, :] = weighted[o * rows:(o + 1) * rows, :]
            turned = stats if o == 0 else pltpu.roll(stats, CHUNK - o * rows, 1)
            send[owner, stat_row:, :] = turned[:, 0:width]
        for o in range(per_chunk):
            owner = chunk * per_chunk + o

            @pl.when(owner != me)
            def _():
                slot = lax.rem(me - owner - 1 + n, n)
                pltpu.make_async_remote_copy(
                    src_ref=send.at[owner], dst_ref=recv.at[slot], send_sem=send_sem, recv_sem=recv_sem,
                    device_id=(owner // ngy, lax.rem(owner, ngy)), device_id_type=MESH).start()
        return top_even

    top_even = score(chunk_of(0), 0, s_even)
    pl.semaphore_wait(barrier, n - 1)
    lax.fori_loop(0, nchunk, one_chunk, top_even)

    recv[n - 1] = send[me]
    most = recv.at[pl.ds(0, n - 1)]
    whole = pltpu.make_async_remote_copy(
        src_ref=most, dst_ref=most, send_sem=send_sem, recv_sem=recv_sem,
        device_id=(gx, gy), device_id_type=MESH)
    whole.wait_send()
    whole.wait_recv()

    tops = recv[:, stat_row, :]
    top = jnp.max(tops, axis=0, keepdims=True)
    factor = jnp.exp(tops - top)
    total = jnp.sum(factor * recv[:, stat_row + 1, :], axis=0, keepdims=True)
    target = jnp.sum(recv[:, stat_row + 2, :], axis=0, keepdims=True)
    nll_out[...] = top + jnp.log(total) - target
    share = (factor / total).T
    out = jnp.zeros((rows, width), jnp.float32)
    for s in range(n):
        out = out + share[0:rows, s:s + 1] * recv[s, 0:rows, :]
    exp_out[...] = out


def solution(mesh):
    n = mesh.size
    ngy = mesh.shape["gy"]

    def local(hidden_states, item_table, targets):
        positions, width = hidden_states.shape
        items = item_table.shape[0]
        rows = positions // n
        held = -(-rows // 8) * 8 + 8
        vmem = pl.BlockSpec(memory_space=pltpu.VMEM)
        expected, nll = pl.pallas_call(
            functools.partial(kernel, n, ngy, rows),
            out_shape=(jax.ShapeDtypeStruct((rows, width), jnp.float32), jax.ShapeDtypeStruct((1, width), jnp.float32)),
            in_specs=[vmem, vmem, vmem],
            out_specs=(vmem, vmem),
            scratch_shapes=[
                pltpu.VMEM((width + 16, items), jnp.bfloat16),
                pltpu.VMEM((BLOCK, CHUNK), jnp.float32),
                pltpu.VMEM((BLOCK, CHUNK), jnp.float32),
                pltpu.VMEM((width + 16, CHUNK), jnp.float32),
                pltpu.VMEM((n, held, width), jnp.float32),
                pltpu.VMEM((n, held, width), jnp.float32),
                pltpu.SemaphoreType.DMA,
                pltpu.SemaphoreType.DMA,
            ],
            compiler_params=pltpu.CompilerParams(collective_id=0, has_side_effects=True, vmem_limit_bytes=60000000),
        )(hidden_states, item_table, targets.reshape(1, positions))
        return expected, nll[0, :rows]

    return jax.shard_map(
        local, mesh=mesh,
        in_specs=(P(), P(AXES, None), P()),
        out_specs=(P(AXES, None), P(AXES)),
        check_vma=False,
    )
```

time: 253 us -> 30.9 us (0.12)
  waiting for transfers between devices: 90.1 us -> 0 us
  blocking collectives: 82.2 us -> 0 us
  matrix products: 51.5 us -> 0 us
  Pallas kernels: 0 us -> 27.6 us
  between operations: 14.1 us -> 0.64 us
  other arithmetic: 8.69 us -> 0 us
    reduce_scatter x1 -> x0, waiting for transfers between devices: 90.1 us -> none  [local(): lax.psum_scatter(weighted * factor[:, None], ('gx', 'gy'), scatter_dimens...]
    dot_general x32 -> x0, matrix products: 51.5 us -> none  [the longest x16 28 us: visit_block(): block_acc = jnp.dot(probs_low, block, preferred_element_type=jnp.float32)]
    pmax x1 -> x0, blocking collectives: 42 us -> none  [local(): global_max = lax.pmax(highest, ('gx', 'gy'))]
    unnamed x1 -> x0, blocking collectives: 40.2 us -> none
    pallas_call x0 -> x1, Pallas kernels: none -> 27.6 us  [local(): pl.pallas_call(functools.partial(kernel, n, ngy, rows), out_shape=(jax.Sh...]
    reduce_sum x17 -> x0, other arithmetic: 5.45 us -> none  [the longest x16 5.24 us: visit_block(): block_sum = jnp.sum(exponent, axis=1)]
    gather x1 -> x0, local copies, waits for them, and re-layouts: 4.74 us -> none  [local(): target_rows = item_table[jnp.clip(local_index, 0, shard_items - 1)]]
  transfers between devices with their start and end apart: 1 -> 0, of which waited for: 1 -> 0; matrix products, arithmetic and copies ran while one was open for 2% -> 0% of each run, Pallas kernels for 0% -> 0%
where the time goes in v1:
time: 30.9 us; the launch traced here: 30.7 us
  Pallas kernels  27.6 us (89%)
  local copies, waits for them, and re-layouts  2.46 us (8%)
  between operations  0.64 us (2%)
    pallas_call x1, Pallas kernels, local(): pl.pallas_call(functools.partial(kernel, n, ngy, rows), out_shape=(jax.Sh...  27.6 us
    unnamed x1, local copies, waits for them, and re-layouts  1.32 us
    squeeze x1, local copies, waits for them, and re-layouts, local(): return (expected, nll[0, :rows])  1.14 us

profile of v1, /device:TPU:0, one launch (start us, length us, event | category | flops | bytes accessed | tf_op | source)
XLA Modules:
  0.0 30.7 jit_solution(17072427673852744318)
XLA Ops:
  0.6 27.6 %shard_map.50 = (f32[32,128]{1,0:T(8,128)}, f32[1,128]{1,0:T(1,128)}) custom-call(bf16[1024,128]{1,0:T(8,128)(2,1)} %hid.1, bf16[8192,128]{1,0:T(8,128)(2,1)} %tab.1, s32[1,1024]{1,0:T(1,128)} %bitcast.3), custom_call_target="tpu_custom_call" | custom-call | tf_op jit(solution)/shard_map/pallas_call | solution.py:153
  28.2 1.1 %slice_bitcast_fusion = f32[32]{0:T(128)} fusion(f32[1,128]{1,0:T(1,128)} %get-tuple-element.5), kind=kLoop, calls=%fused_computation | loop fusion | bytes 256 | tf_op jit(solution)/shard_map/squeeze | solution.py:170
  29.4 1.3 %copy.6 = f32[32,128]{1,0:T(8,128)} copy(f32[32,128]{1,0:T(8,128)} %get-tuple-element.8) | data formatting | bytes 32768

commit v2 on v1

v2 whole, which is shorter than its diff:
```python
import functools

import jax
import jax.numpy as jnp
from jax import lax
from jax.experimental import pallas as pl
from jax.experimental.pallas import tpu as pltpu
from jax.sharding import PartitionSpec as P

AXES = ("gx", "gy")
BLOCK = 4096
SUB = 256
PARTS = 8
DEPTH = 512
MESH = pl.DeviceIdType.MESH
NT = (((1,), (1,)), ((), ()))


def kernel(ngx, ngy, rows, hid, table, tgt, packed,
           tab, tabt, held, acc, give, take, send, recv, give_sem, take_sem, send_sem, recv_sem, load_sem):
    CHUNK = rows * ngy
    positions, width = hid.shape
    items = table.shape[0]
    part = items // PARTS
    loads = []
    for i in range(PARTS):
        at = pl.ds(i * part, part)
        loads.append(pltpu.make_async_copy(table.at[at], tab.at[at], load_sem.at[i]))
        loads[i].start()
    nchunk = positions // CHUNK
    nblock = items // BLOCK
    stat_row = send.shape[1] - 8
    gx = lax.axis_index("gx")
    gy = lax.axis_index("gy")
    me = gx * ngy + gy
    core, line = lax.rem(gx, 2), gx // 2
    half = ngx // 2 * ngy
    place_of_me = line * ngy + gy
    partner = (gx + 1 - 2 * core, gy)

    barrier = pltpu.get_barrier_semaphore()

    def greet(k, c):
        other = lax.rem(place_of_me + k, half)
        pl.semaphore_signal(barrier, inc=1, device_id=(other // ngy * 2 + core, lax.rem(other, ngy)), device_id_type=MESH)
        return c

    lax.fori_loop(1, half, greet, 0)
    pl.semaphore_signal(barrier, inc=1, device_id=partner, device_id_type=MESH)

    def turn(base, count):
        at = pl.ds(base, count)
        tabt[0:width, at] = tab[at, :].T

    tabt[width:, :] = jnp.ones((tabt.shape[0] - width, items), jnp.bfloat16)

    sub_iota = lax.broadcasted_iota(jnp.int32, (8, CHUNK), 0)

    def chunk_of(k):
        mine = lax.rem(k, 2)
        return lax.rem(line + 1 + k // 2, nchunk // 2) * 2 + mine * core + (1 - mine) * (1 - core)

    def score(chunk, block, sub):
        at = pl.multiple_of(chunk * CHUNK, CHUNK)
        base = pl.multiple_of(block * BLOCK + sub * SUB, SUB)
        s = lax.dot_general(tab[pl.ds(base, SUB), :], hid[pl.ds(at, CHUNK), :], NT, preferred_element_type=jnp.float32)
        held[sub * SUB:(sub + 1) * SUB, :] = s
        return functools.reduce(jnp.maximum, [s[8 * g:8 * g + 8] for g in range(SUB // 8)])

    def top_of(tops):
        return jnp.max(functools.reduce(jnp.maximum, tops), axis=0, keepdims=True)

    def step(k, place, turning, j, carry):
        top, highest, hit = carry
        new = jnp.maximum(highest, top)
        retain = jnp.exp(highest - new)
        here = place - j * BLOCK
        later = k * nblock + j + 1
        chunk, block = chunk_of(later // nblock), lax.rem(later, nblock)
        tops, added = [], None
        for q in range(BLOCK // DEPTH):
            base = pl.multiple_of(j * BLOCK + q * DEPTH, DEPTH)
            if turning:
                turn(base, DEPTH)
            s = held[q * DEPTH:(q + 1) * DEPTH, :]
            for g in range(DEPTH // 8):
                hit = jnp.where(here == q * DEPTH + 8 * g, s[8 * g:8 * g + 8], hit)
            p = jnp.exp(s - new).astype(jnp.bfloat16)
            part = jnp.dot(tabt[:, pl.ds(base, DEPTH)], p, preferred_element_type=jnp.float32)
            added = part if added is None else added + part
            for sub in range(q * DEPTH // SUB, (q + 1) * DEPTH // SUB):
                tops.append(score(chunk, block, sub))
        acc[...] = acc[...] * retain + added
        return top_of(tops), new, hit

    def one_chunk(turning, k, top):
        chunk = chunk_of(k)
        at = pl.multiple_of(chunk * CHUNK, CHUNK)
        place = tgt[0:1, pl.ds(at, CHUNK)] - me * items - sub_iota
        acc[...] = jnp.zeros_like(acc)
        top, highest, hit = lax.fori_loop(
            0, nblock, functools.partial(step, k, place, turning),
            (top, jnp.full((1, CHUNK), -1e30, jnp.float32), jnp.zeros((8, CHUNK), jnp.float32)))
        return top, highest, jnp.sum(hit, axis=0, keepdims=True)

    def passing(k):
        return pltpu.make_async_remote_copy(
            src_ref=give.at[k // 2], dst_ref=take.at[k // 2], send_sem=give_sem.at[k // 2], recv_sem=take_sem.at[k // 2],
            device_id=partner, device_id_type=MESH)

    def two_chunks(turning, kk, top):
        top, highest, hit = one_chunk(turning, 2 * kk, top)
        give[kk, 0:width + 8, :] = acc[0:width + 8, :]
        give[kk, width + 8:, :] = jnp.concatenate([highest, hit, jnp.zeros((6, CHUNK), jnp.float32)], axis=0)
        passing(2 * kk).start()
        top, highest, hit = one_chunk(False, 2 * kk + 1, top)
        passing(2 * kk).wait_recv()
        other = take[kk, width + 8:width + 9, :]
        both = jnp.maximum(highest, other)
        own_share, other_share = jnp.exp(highest - both), jnp.exp(other - both)
        weighted = (acc[0:width, :] * own_share + take[kk, 0:width, :] * other_share).T
        total = acc[width:width + 1, :] * own_share + take[kk, width:width + 1, :] * other_share
        stats = jnp.concatenate(
            [both, total, hit + take[kk, width + 9:width + 10, :], jnp.zeros((5, CHUNK), jnp.float32)], axis=0)
        chunk = chunk_of(2 * kk + 1)
        for o in range(ngy):
            owner = chunk // 2 * ngy + o
            send[owner, 0:rows, :] = weighted[o * rows:(o + 1) * rows, :]
            turned = stats if o == 0 else pltpu.roll(stats, CHUNK - o * rows, 1)
            send[owner, stat_row:, :] = turned[:, 0:width]
        for o in range(ngy):
            owner = chunk // 2 * ngy + o

            @pl.when(owner != place_of_me)
            def _():
                slot = lax.rem(place_of_me - owner - 1 + half, half)
                pltpu.make_async_remote_copy(
                    src_ref=send.at[owner], dst_ref=recv.at[slot], send_sem=send_sem, recv_sem=recv_sem,
                    device_id=(chunk, o), device_id_type=MESH).start()
        return top

    tops = []
    for i in range(PARTS):
        loads[i].wait()
        tops += [score(chunk_of(0), 0, sub) for sub in range(BLOCK // SUB) if sub * SUB // part == i]
    top = top_of(tops)
    pl.semaphore_wait(barrier, half)
    top = two_chunks(True, 0, top)
    lax.fori_loop(1, nchunk // 2, functools.partial(two_chunks, False), top)

    def given(kk, c):
        passing(2 * kk).wait_send()
        return c

    lax.fori_loop(0, nchunk // 2, given, 0)
    recv[half - 1] = send[place_of_me]
    most = recv.at[pl.ds(0, half - 1)]
    whole = pltpu.make_async_remote_copy(
        src_ref=most, dst_ref=most, send_sem=send_sem, recv_sem=recv_sem,
        device_id=(gx, gy), device_id_type=MESH)
    whole.wait_send()
    whole.wait_recv()

    tops = recv[:, stat_row, :]
    top = jnp.max(tops, axis=0, keepdims=True)
    factor = jnp.exp(tops - top)
    total = jnp.sum(factor * recv[:, stat_row + 1, :], axis=0, keepdims=True)
    target = jnp.sum(recv[:, stat_row + 2, :], axis=0, keepdims=True)
    packed[stat_row:stat_row + 1, :] = top + jnp.log(total) - target
    share = (factor / total).T
    out = jnp.zeros((rows, width), jnp.float32)
    for s in range(half):
        out = out + share[0:rows, s:s + 1] * recv[s, 0:rows, :]
    packed[0:rows, :] = out


def unpack(rows, stat_row, packed, exp_out, nll_out):
    exp_out[...] = packed[0:rows, :]
    nll_out[...] = packed[stat_row, 0:rows]


def solution(mesh):
    n = mesh.size
    ngx, ngy = mesh.shape["gx"], mesh.shape["gy"]

    def local(hidden_states, item_table, targets):
        positions, width = hidden_states.shape
        items = item_table.shape[0]
        rows = positions // n
        chunk = rows * ngy
        tall = -(-rows // 8) * 8 + 8
        vmem = pl.BlockSpec(memory_space=pltpu.VMEM)
        packed = pl.pallas_call(
            functools.partial(kernel, ngx, ngy, rows),
            out_shape=jax.ShapeDtypeStruct((tall, width), jnp.float32),
            in_specs=[vmem, pl.BlockSpec(memory_space=pl.ANY), vmem],
            out_specs=vmem,
            scratch_shapes=[
                pltpu.VMEM((items, width), jnp.bfloat16),
                pltpu.VMEM((width + 16, items), jnp.bfloat16),
                pltpu.VMEM((BLOCK, chunk), jnp.float32),
                pltpu.VMEM((width + 16, chunk), jnp.float32),
                pltpu.VMEM((ngx // 2, width + 16, chunk), jnp.float32),
                pltpu.VMEM((ngx // 2, width + 16, chunk), jnp.float32),
                pltpu.VMEM((n // 2, tall, width), jnp.float32),
                pltpu.VMEM((n // 2, tall, width), jnp.float32),
                pltpu.SemaphoreType.DMA((ngx // 2,)),
                pltpu.SemaphoreType.DMA((ngx // 2,)),
                pltpu.SemaphoreType.DMA,
                pltpu.SemaphoreType.DMA,
                pltpu.SemaphoreType.DMA((PARTS,)),
            ],
            compiler_params=pltpu.CompilerParams(collective_id=0, has_side_effects=True, vmem_limit_bytes=60000000),
        )(hidden_states, item_table, targets.reshape(1, positions))
        return pl.pallas_call(
            functools.partial(unpack, rows, tall - 8),
            out_shape=(jax.ShapeDtypeStruct((rows, width), jnp.float32), jax.ShapeDtypeStruct((rows,), jnp.float32)),
            in_specs=[vmem], out_specs=(vmem, vmem),
        )(packed)

    return jax.shard_map(
        local, mesh=mesh,
        in_specs=(P(), P(AXES, None), P()),
        out_specs=(P(AXES, None), P(AXES)),
        check_vma=False,
    )
```

time: 30.9 us -> 24.9 us (0.81)
  Pallas kernels: 27.6 us -> 24.1 us
  local copies, waits for them, and re-layouts: 2.46 us -> 0 us
    pallas_call x1 -> x2, Pallas kernels: 27.6 us -> 24.1 us  [the longest x1 22.7 us: local(): pl.pallas_call(functools.partial(kernel, ngx, ngy, rows), out_shape=jax.S...]
    unnamed x1 -> x0, local copies, waits for them, and re-layouts: 1.32 us -> none
    squeeze x1 -> x0, local copies, waits for them, and re-layouts: 1.14 us -> none  [local(): return (expected, nll[0, :rows])]
where the time goes in v2:
time: 24.9 us; the launch traced here: 24.7 us
  Pallas kernels  24.1 us (97%)
  between operations  0.64 us (3%)
    pallas_call x1, Pallas kernels, local(): pl.pallas_call(functools.partial(kernel, ngx, ngy, rows), out_shape=jax.S...  22.7 us
    pallas_call x1, Pallas kernels, local(): pl.pallas_call(functools.partial(unpack, rows, tall - 8), out_shape=(jax....  1.34 us

profile of v2, /device:TPU:0, one launch (start us, length us, event | category | flops | bytes accessed | tf_op | source)
XLA Modules:
  0.0 24.7 jit_solution(18091494230493487487)
XLA Ops:
  0.6 22.7 %shard_map.50.packed = f32[40,128]{1,0:T(8,128)} custom-call(bf16[1024,128]{1,0:T(8,128)(2,1)} %hid.1, bf16[8192,128]{1,0:T(8,128)(2,1)} %table.1, s32[1,1024]{1,0:T(1,128)} %bitcast.1), custom_call_target="tpu_custom_call" | custom-call | tf_op jit(solution)/shard_map/pallas_call | solution.py:193
  23.4 1.3 %shard_map.51 = (f32[32,128]{1,0:T(8,128)}, f32[32]{0:T(128)}) custom-call(f32[40,128]{1,0:T(8,128)} %shard_map.50.packed), custom_call_target="tpu_custom_call" | custom-call | tf_op jit(solution)/shard_map/pallas_call | solution.py:215
